TPU v7x, 256 devices: a 2x2x32 block of a 4x8x32 slice. The times are simulated.
256 devices in a mesh: parts: 4 (over x, y), owner: 64 (over z, core).
Axes of the slice: x: 2, y: 2, z: 32, core: 2. Of those that a mesh axis runs over, the one named last changes fastest.
The devices are a block of a 4x8x32 slice.
Arguments:
- embeddings: bfloat16 [1048576, 512], P(('parts', 'owner')), parts along dimension 0, may hold values from -6 to 6
- cluster: int32 [1048576], P(('parts', 'owner')), parts along dimension 0, may hold values from 0 to 7
- lengths: int32 [256, 64], P(('parts', 'owner')), parts along dimension 0, may hold values from 1 to 64, 3584 in all within a row
Outputs:
- best: float32 [1048576], P(('parts', 'owner')), parts along dimension 0
There are 4 independent parts, one for each index of `parts`. A program takes and returns all parts, laid end to end along the dimension named above; each array names one. Nothing has to cross between parts.
Inputs may be any that keep to these rules, and one draw needn't show every extreme that they name: Each row of lengths sums to 3584 and reaches 64 in some column.
All inputs are finite; a program needn't handle non-finite values.
Results may differ from a plain program's by a relative error of at most 0.00049.
Values may be sent and summed in bfloat16 or wider, within the bound.
A program may use at most 64 MiB of HBM per device.

v0:
```python
import math

import jax
import jax.numpy as jnp
from jax import lax
from jax.sharding import PartitionSpec as P


def normalize(embeddings, width):
    values = embeddings.astype(jnp.float32)
    factor = lax.rsqrt(jnp.mean(values * values, axis=-1, keepdims=True) + 1e-06) / math.sqrt(width)
    return (values * factor).astype(jnp.bfloat16)


def block_best(block_units, block_labels, first, units, labels):
    similar = jnp.einsum("ie,je->ij", block_units, units, preferred_element_type=jnp.float32)
    rows_index = first + jnp.arange(block_units.shape[0], dtype=jnp.int32)
    cols_index = jnp.arange(units.shape[0], dtype=jnp.int32)
    same_group = (
        (block_labels[:, None] == labels[None, :])
        & (block_labels[:, None] >= 0)
        & (rows_index[:, None] != cols_index[None, :])
    )
    return jnp.max(jnp.where(same_group, similar, jnp.float32(-1.0)), axis=1)


def on_device(embeddings, cluster, lengths):
    owners = lax.axis_size("owner")
    rows_here, width = embeddings.shape
    capacity = rows_here // owners
    units = normalize(embeddings, width)
    slots = jnp.arange(rows_here, dtype=jnp.int32)
    limits = jnp.repeat(lengths[0], capacity, total_repeat_length=rows_here)
    live = slots % capacity < limits
    labels = jnp.where(live, cluster, -1).astype(jnp.bfloat16)
    got_units, got_labels = (
        lax.all_to_all(units, "owner", split_axis=0, concat_axis=0, tiled=True),
        lax.all_to_all(labels, "owner", split_axis=0, concat_axis=0, tiled=True),
    )
    got_labels = got_labels.astype(jnp.int32)
    block_rows = min(512, rows_here)
    block_count = rows_here // block_rows

    def one_block(pair):
        index, block_units, block_labels = pair
        return block_best(block_units, block_labels, index * block_rows, got_units, got_labels)

    found = lax.map(
        one_block,
        (
            jnp.arange(block_count, dtype=jnp.int32),
            got_units.reshape(block_count, block_rows, width),
            got_labels.reshape(block_count, block_rows),
        ),
    )
    found = found.reshape(rows_here)
    answer = lax.all_to_all(found, "owner", split_axis=0, concat_axis=0, tiled=True)
    return answer


def solution(mesh):
    return jax.shard_map(
        on_device,
        mesh=mesh,
        in_specs=(P(("parts", "owner"), None), P(("parts", "owner")), P(("parts", "owner"), None)),
        out_specs=P(("parts", "owner")),
        check_vma=False,
    )
```

profile of v0, /device:TPU:46, one launch (start us, length us, event | category | flops | bytes accessed | tf_op | source)
XLA Modules:
  0.0 581.4 jit_solution(16393098511606007399)
XLA Ops:
  0.0 2.1 fusion.10
  2.1 1.6 fusion.13
  3.7 2.1 fusion.12
  5.8 2.1 fusion.11
  7.8 0.8 add_add_fusion.1
  8.6 4.3 compare_select_fusion.1
  12.9 2.9 compare_reduce_fusion.56
  15.9 36.5 %select_convert_fusion = bf16[4096]{0:T(1024)(128)(2,1)S(1)} fusion(s32[4096]{0:T(1024)} %param.8, pred[4096]{0:T(1024)(128)(4,1)S(1)} %get-tuple-element.111, pred[4096]{0:T(1024)(128)(4,1)S(1)} %get-tuple-element.110, pred[4096]{0:T(1024)(128)(4,1)S(1)} %get-tuple-element.109, pred[4096]{0:T(1024)(128)(4,1)S(1)} %get-tuple-element.108, ...), kind=kLoop, calls=%fused_computation.84 | loop fusion | flops 307200 | bytes 291172 | tf_op jit(solution)/shard_map/convert_element_type | solution.py:35
  52.3 0.7 all_to_all.30
  53.0 34.2 %all-to-all-start = ((bf16[64,64,1]{1,2,0:T(2,128)(2,1)}), bf16[64,64,1]{1,2,0:T(2,128)(2,1)S(1)}, u32[]{:S(2)}, u32[]{:S(2)}) async-start(bf16[64,64,1]{1,2,0:T(2,128)(2,1)} %all_to_all.30), calls=%async_computation | async-start | bytes 65536 | tf_op jit(solution)/shard_map/all_to_all | solution.py:38
  87.3 3.2 fusion.4
  90.5 0.2 copy-done
  90.7 2.4 fusion.5
  93.1 16.1 %all-to-all-done = bf16[64,64,1]{1,2,0:T(2,128)(2,1)S(1)} async-done(((bf16[64,64,1]{1,2,0:T(2,128)(2,1)}), bf16[64,64,1]{1,2,0:T(2,128)(2,1)S(1)}, u32[]{:S(2)}, u32[]{:S(2)}) %all-to-all-start) | async-done | bytes 8224 | tf_op jit(solution)/shard_map/all_to_all | solution.py:38
  109.2 7.5 %all-to-all-start.1 = ((bf16[64,64,512]{2,1,0:T(8,128)(2,1)}), bf16[64,64,512]{2,1,0:T(8,128)(2,1)}, u32[]{:S(2)}, u32[]{:S(2)}) async-start(bf16[64,64,512]{2,1,0:T(8,128)(2,1)} %bitcast.101), calls=%async_computation.1 | async-start | bytes 8388608 | tf_op jit(solution)/shard_map/all_to_all | solution.py:37
  116.7 0.1 convert_reduce_fusion
  116.9 0.1 reshape.125
  117.0 0.1 reshape.126
  117.0 378.4 %all-to-all-done.1 = bf16[64,64,512]{2,1,0:T(8,128)(2,1)} async-done(((bf16[64,64,512]{2,1,0:T(8,128)(2,1)}), bf16[64,64,512]{2,1,0:T(8,128)(2,1)}, u32[]{:S(2)}, u32[]{:S(2)}) %all-to-all-start.1) | async-done | bytes 4194336 | tf_op jit(solution)/shard_map/all_to_all | solution.py:37
  495.4 56.3 %while.11 = (s32[]{:T(128)}, f32[8,512]{1,0:T(8,128)S(1)}, s32[8,512]{1,0:T(8,128)S(1)}, s32[4096]{0:T(1024)S(1)}, s32[8]{0:T(128)S(1)}, /*index=5*/bf16[8,512,5...) while((s32[]{:T(128)}, f32[8,512]{1,0:T(8,128)S(1)}, ...), condition=%wide.region_3.4_spmd, body=%wide.region_1.0_spmd.sunk | while | flops 2160067072 | bytes 4755081 | solution.py:48
  495.4 0.6 dynamic_slice.22
  496.7 5.7 select_reduce_fusion.2
  502.4 0.1 dynamic_update_slice.5
  502.5 0.6 dynamic_slice.22
  503.7 5.7 select_reduce_fusion.2
  509.4 0.1 dynamic_update_slice.5
  509.5 0.6 dynamic_slice.22
  510.8 5.7 select_reduce_fusion.2
  516.4 0.1 dynamic_update_slice.5
  516.5 0.6 dynamic_slice.22
  517.8 5.7 select_reduce_fusion.2
  523.5 0.1 dynamic_update_slice.5
  523.6 0.6 dynamic_slice.22
  524.8 5.7 select_reduce_fusion.2
  530.5 0.1 dynamic_update_slice.5
  530.6 0.6 dynamic_slice.22
  531.8 5.7 select_reduce_fusion.2
  537.5 0.1 dynamic_update_slice.5
  537.6 0.6 dynamic_slice.22
  538.9 5.7 select_reduce_fusion.2
  544.6 0.1 dynamic_update_slice.5
  544.7 0.6 dynamic_slice.22
  545.9 5.7 select_reduce_fusion.2
  551.7 0.1 all_to_all.27
  551.8 27.7 %all_to_all.34 = f32[64,64,1]{1,2,0:T(1,128)S(1)} all-to-all(f32[64,64,1]{1,2,0:T(1,128)S(1)} %all_to_all.27), channel_id=1, replica_groups=mesh['parts'=4,'owner'=64] {'owner'}, dimensions={0} | all-to-all | bytes 32768 | tf_op jit(solution)/shard_map/all_to_all | solution.py:57
  579.4 0.5 broadcast.588
  580.0 0.7 reduce.125
  580.7 0.7 all_to_all.29
  (31 shorter events, 0.3 us)
Async XLA Ops:
  53.0 56.2 %all-to-all-start = ((bf16[64,64,1]{1,2,0:T(2,128)(2,1)}), bf16[64,64,1]{1,2,0:T(2,128)(2,1)S(1)}, u32[]{:S(2)}, u32[]{:S(2)}) async-start(bf16[64,64,1]{1,2,0:T(2,128)(2,1)} %all_to_all.30), calls=%async_computation | async-start | bytes 65536 | tf_op jit(solution)/shard_map/all_to_all | solution.py:38
  87.3 3.5 copy-start
  109.2 386.2 %all-to-all-start.1 = ((bf16[64,64,512]{2,1,0:T(8,128)(2,1)}), bf16[64,64,512]{2,1,0:T(8,128)(2,1)}, u32[]{:S(2)}, u32[]{:S(2)}) async-start(bf16[64,64,512]{2,1,0:T(8,128)(2,1)} %bitcast.101), calls=%async_computation.1 | async-start | bytes 8388608 | tf_op jit(solution)/shard_map/all_to_all | solution.py:37
where the time goes:
time: 583 us; the launch traced here: 581 us
  waiting for transfers between devices  394 us (68%)
  other arithmetic  51.1 us (9%)
  matrix products  45.5 us (8%)
  starting transfers between devices  41.7 us (7%)
  blocking collectives  27.7 us (5%)
  local copies, waits for them, and re-layouts  15.4 us (3%)
    all_to_all x1, waiting for transfers between devices, on_device(): lax.all_to_all(units, 'owner', split_axis=0, concat_axis=0, tiled=True)  378 us
    dot_general x8, matrix products, block_best(): jnp.einsum('ie,je->ij', block_units, units, preferred_element_type=jnp.fl...  45.5 us
    convert_element_type x1, other arithmetic, on_device(): labels = jnp.where(live, cluster, -1).astype(jnp.bfloat16)  36.5 us
    all_to_all x1, starting transfers between devices, on_device(): lax.all_to_all(labels, 'owner', split_axis=0, concat_axis=0, tiled=True)  34.2 us
    all_to_all x1, blocking collectives, on_device(): lax.all_to_all(found, 'owner', split_axis=0, concat_axis=0, tiled=True)  27.7 us
    all_to_all x1, waiting for transfers between devices, on_device(): lax.all_to_all(labels, 'owner', split_axis=0, concat_axis=0, tiled=True)  16.1 us
  transfers between devices with their start and end apart: 2, of which 2 were waited for; matrix products, arithmetic and copies ran while one was open for 1% of the time, Pallas kernels for 0%

commit v1 on v0

v1 whole, which is shorter than its diff:
```python
import math

import jax
import jax.numpy as jnp
from jax import lax
from jax.experimental import pallas as pl
from jax.experimental.pallas import tpu as pltpu
from jax.sharding import PartitionSpec as P

AHEAD = 16
GROUP = 4
OWNER = "owner"


def exchange_kernel(
    owners, emb_hbm, lab_ref, out_ref,
    emb_v, land, units, lab_land, labrow, labcol, rowacc, colbest, res_out, res_land,
    load_sem, self_sem, send_sem, recv_sem, lab_send, lab_recv, res_send, res_recv,
):
    chips = owners // 2
    far = chips // 2
    cap = land.shape[1]
    width = land.shape[2]
    tile = 4 * cap
    half_tile = 2 * cap
    me = lax.axis_index(OWNER)
    core = lax.rem(me, 2)
    chip = me // 2

    load = pltpu.make_async_copy(emb_hbm, emb_v, load_sem)
    load.start()

    barrier = pltpu.get_barrier_semaphore()

    def greet(i, _):
        pl.semaphore_signal(barrier, inc=1, device_id={OWNER: lax.rem(me + i, owners)})
        return 0

    lax.fori_loop(1, owners, greet, 0)

    labcol[...] = jnp.full_like(labcol, -2)
    rowacc[...] = jnp.full_like(rowacc, -1.0)

    pl.semaphore_wait(barrier, owners - 1)
    load.wait()

    def block_copy(dest, slot, land_slot):
        return pltpu.make_async_remote_copy(
            src_ref=emb_v.at[pl.ds(pl.multiple_of(dest * cap, cap), cap)],
            dst_ref=land.at[land_slot],
            send_sem=send_sem.at[slot],
            recv_sem=recv_sem.at[land_slot],
            device_id={OWNER: dest},
        )

    def label_copy(dest, slot, land_slot):
        return pltpu.make_async_remote_copy(
            src_ref=lab_ref.at[dest],
            dst_ref=lab_land.at[land_slot],
            send_sem=lab_send.at[slot],
            recv_sem=lab_recv.at[land_slot],
            device_id={OWNER: dest},
        )

    def start(dest, slot, land_slot):
        label_copy(dest, slot, land_slot).start()
        block_copy(dest, slot, land_slot).start()

    def send_phase(t):
        k = far - t
        right = lax.rem(chip + k, chips)
        left = lax.rem(chip + chips - k, chips)
        for c in range(2):
            start(right * 2 + c, t * 4 + c, t * 4 + core)
            start(left * 2 + c, t * 4 + 2 + c, t * 4 + 2 + core)

    keep = pltpu.make_async_copy(
        emb_v.at[pl.ds(pl.multiple_of(me * cap, cap), cap)], land.at[core], self_sem.at[0])
    keep_lab = pltpu.make_async_copy(lab_ref.at[me], lab_land.at[core], self_sem.at[1])
    keep.start()
    keep_lab.start()
    partner = chip * 2 + 1 - core
    start(partner, 0, core)
    opposite = lax.rem(chip + far, chips)
    for c in range(2):
        start(opposite * 2 + c, 2 + c, 2 + core)

    def issue(t, _):
        send_phase(t)
        return 0

    lax.fori_loop(1, min(AHEAD, far), issue, 0)

    def arrived(slot):
        label_copy(me, slot, slot).wait_recv()
        block_copy(me, slot, slot).wait_recv()

    def best_of(t):
        for h in range(2):
            row = jnp.maximum(lab_land[4 * t + 2 * h], lab_land[4 * t + 2 * h + 1])
            labrow[2 * t + h] = row
            spread = jnp.broadcast_to(row, (half_tile, half_tile))
            column = jnp.transpose(spread)
            labcol[pl.ds(pl.multiple_of(t * tile + h * half_tile, half_tile), half_tile), :] = jnp.where(
                column < 0, -2, column)
        values = land[pl.ds(4 * t, 4)].reshape(tile, width).astype(jnp.float32)
        factor = lax.rsqrt(jnp.mean(values * values, axis=-1, keepdims=True) + 1e-06) / math.sqrt(width)
        new = (values * factor).astype(jnp.bfloat16)
        units[pl.ds(pl.multiple_of(t * tile, tile), tile), :] = new

        def group(g, running, diagonal):
            span = GROUP * tile
            rows = pl.ds(pl.multiple_of(g * span, span), span)
            old = units[rows, :]
            fresh = units[pl.ds(pl.multiple_of(t * tile, tile), tile), :]
            sim = lax.dot_general(
                old, fresh, (((1,), (1,)), ((), ())), preferred_element_type=jnp.float32)
            col = labcol[rows, :]
            acc = rowacc[rows, :]
            out = []
            for h in range(2):
                part = sim[:, h * half_tile:(h + 1) * half_tile]
                same = col == labrow[2 * t + h]
                if diagonal:
                    i = g * span + lax.broadcasted_iota(jnp.int32, part.shape, 0)
                    j = t * tile + h * half_tile + lax.broadcasted_iota(jnp.int32, part.shape, 1)
                    same = same & (i != j)
                part = jnp.where(same, part, -1.0)
                acc = jnp.maximum(acc, part)
                out.append(jnp.maximum(running[h], jnp.max(part, axis=0, keepdims=True)))
            rowacc[rows, :] = acc
            return tuple(out)

        floor = jnp.full((1, half_tile), -1.0, jnp.float32)
        running = lax.fori_loop(0, t // GROUP, lambda g, r: group(g, r, False), (floor, floor))
        running = group(t // GROUP, running, True)
        for h in range(2):
            colbest[2 * t + h] = running[h]

    keep.wait()
    keep_lab.wait()
    arrived(1 - core)
    arrived(2)
    arrived(3)
    best_of(0)

    def step(t, _):
        @pl.when(t + AHEAD - 1 < far)
        def _():
            send_phase(t + AHEAD - 1)
        for s in range(4):
            arrived(4 * t + s)
        best_of(t)
        return 0

    lax.fori_loop(1, far, step, 0)

    def finish(i, _):
        block = rowacc[pl.ds(pl.multiple_of(i * half_tile, half_tile), half_tile), :]
        late = jnp.max(jnp.transpose(block), axis=0, keepdims=True)
        res_out[i] = jnp.maximum(colbest[i], late)
        return 0

    lax.fori_loop(0, chips, finish, 0)

    def result_copy(row, dest, slot):
        return pltpu.make_async_remote_copy(
            src_ref=res_out.at[row],
            dst_ref=res_land.at[me],
            send_sem=res_send.at[slot],
            recv_sem=res_recv.at[me],
            device_id={OWNER: dest},
        )

    for c in range(2):
        result_copy(1, opposite * 2 + c, 2 + c).start()

    def give(t, _):
        k = far - t
        right = lax.rem(chip + k, chips)
        left = lax.rem(chip + chips - k, chips)
        for c in range(2):
            result_copy(2 * t, left * 2 + c, t * 4 + c).start()
            result_copy(2 * t + 1, right * 2 + c, t * 4 + 2 + c).start()
        return 0

    lax.fori_loop(1, far, give, 0)
    result_copy(0, partner, 0).start()
    res_land[me] = res_out[0]

    def back(i, _):
        s = lax.rem(me + i, owners)
        pltpu.make_async_remote_copy(
            src_ref=res_out.at[0], dst_ref=res_land.at[s], send_sem=res_send.at[0],
            recv_sem=res_recv.at[s], device_id={OWNER: s},
        ).wait_recv()
        return 0

    lax.fori_loop(1, owners, back, 0)

    lane = lax.broadcasted_iota(jnp.int32, (1, half_tile), 1)
    for k in range(chips):
        low, high = res_land[2 * k], res_land[2 * k + 1]
        low = jnp.where(core == 0, low, pltpu.roll(low, cap, 1))
        high = jnp.where(core == 0, pltpu.roll(high, cap, 1), high)
        out_ref[k:k + 1, :] = jnp.where(lane < cap, low, high)

    def sent(slot, _):
        block_copy(me, slot, slot).wait_send()
        label_copy(me, slot, slot).wait_send()
        result_copy(0, me, slot).wait_send()
        return 0

    sent(0, 0)
    lax.fori_loop(2, owners, sent, 0)


def on_device(embeddings, cluster, lengths):
    owners = lax.axis_size(OWNER)
    rows_here, width = embeddings.shape
    cap = rows_here // owners
    chips = owners // 2
    core = lax.rem(lax.axis_index(OWNER), 2)
    slot = lax.broadcasted_iota(jnp.int32, (owners, cap), 1)
    labels = jnp.where(slot < lengths.reshape(owners, 1), cluster.reshape(owners, cap), -1)
    lane = lax.broadcasted_iota(jnp.int32, (owners, 2 * cap), 1)
    both = jnp.concatenate([labels, labels], axis=1)
    mine = jnp.where((lane >= cap) == (core == 1), both, -1)[:, None, :]
    dma = pltpu.SemaphoreType.DMA
    out = pl.pallas_call(
        lambda *refs: exchange_kernel(owners, *refs),
        out_shape=jax.ShapeDtypeStruct((chips, 2 * cap), jnp.float32),
        in_specs=[pl.BlockSpec(memory_space=pl.ANY), pl.BlockSpec(memory_space=pltpu.VMEM)],
        out_specs=pl.BlockSpec(memory_space=pltpu.VMEM),
        scratch_shapes=[
            pltpu.VMEM((rows_here, width), jnp.bfloat16),
            pltpu.VMEM((owners, cap, width), jnp.bfloat16),
            pltpu.VMEM((rows_here, width), jnp.bfloat16),
            pltpu.VMEM((owners, 1, 2 * cap), jnp.int32),
            pltpu.VMEM((chips, 1, 2 * cap), jnp.int32),
            pltpu.VMEM((rows_here, 2 * cap), jnp.int32),
            pltpu.VMEM((rows_here, 2 * cap), jnp.float32),
            pltpu.VMEM((chips, 1, 2 * cap), jnp.float32),
            pltpu.VMEM((chips, 1, 2 * cap), jnp.float32),
            pltpu.VMEM((owners, 1, 2 * cap), jnp.float32),
            dma, dma((2,)),
            dma((owners,)), dma((owners,)), dma((owners,)), dma((owners,)), dma((owners,)), dma((owners,)),
        ],
        compiler_params=pltpu.CompilerParams(
            collective_id=0, has_side_effects=True, vmem_limit_bytes=48 << 20),
        cost_estimate=pl.CostEstimate(
            flops=2 * rows_here * rows_here * width, bytes_accessed=4 * rows_here * width, transcendentals=0),
    )(embeddings, mine)
    return out.reshape(rows_here)


def solution(mesh):
    return jax.shard_map(
        on_device,
        mesh=mesh,
        in_specs=(P(("parts", OWNER), None), P(("parts", OWNER)), P(("parts", OWNER), None)),
        out_specs=P(("parts", OWNER)),
        check_vma=False,
    )
```

time: 583 us -> 429 us (0.74)
  Pallas kernels: 0 us -> 423 us
  waiting for transfers between devices: 394 us -> 0 us
  other arithmetic: 51.1 us -> 0.87 us
  matrix products: 45.5 us -> 0 us
  starting transfers between devices: 41.7 us -> 0 us
  blocking collectives: 27.7 us -> 0 us
  local copies, waits for them, and re-layouts: 15.4 us -> 3.58 us
    pallas_call x0 -> x1, Pallas kernels: none -> 423 us  [on_device(): pl.pallas_call(lambda *refs: exchange_kernel(owners, *refs), out_shape=ja...]
    all_to_all x2 -> x0, waiting for transfers between devices: 394 us -> none  [the longest x1 378 us: on_device(): lax.all_to_all(units, 'owner', split_axis=0, concat_axis=0, tiled=True)]
    dot_general x8 -> x0, matrix products: 45.5 us -> none  [block_best(): jnp.einsum('ie,je->ij', block_units, units, preferred_element_type=jnp.fl...]
    all_to_all x2 -> x0, starting transfers between devices: 41.7 us -> none  [the longest x1 34.2 us: on_device(): lax.all_to_all(labels, 'owner', split_axis=0, concat_axis=0, tiled=True)]
    convert_element_type x4 -> x0, other arithmetic: 39.1 us -> none  [the longest x1 36.5 us: on_device(): labels = jnp.where(live, cluster, -1).astype(jnp.bfloat16)]
    all_to_all x1 -> x0, blocking collectives: 27.7 us -> none  [on_device(): lax.all_to_all(found, 'owner', split_axis=0, concat_axis=0, tiled=True)]
    gather x4 -> x0, local copies, waits for them, and re-layouts: 7.81 us -> none  [on_device(): limits = jnp.repeat(lengths[0], capacity, total_repeat_length=rows_here)]
    gather x2 -> x0, other arithmetic: 7.22 us -> none  [on_device(): limits = jnp.repeat(lengths[0], capacity, total_repeat_length=rows_here)]
  transfers between devices with their start and end apart: 2 -> 0, of which waited for: 2 -> 0; matrix products, arithmetic and copies ran while one was open for 1% -> 0% of each run, Pallas kernels for 0% -> 0%
where the time goes in v1:
time: 429 us; the launch traced here: 428 us
  Pallas kernels  423 us (99%)
    pallas_call x1, Pallas kernels, on_device(): pl.pallas_call(lambda *refs: exchange_kernel(owners, *refs), out_shape=ja...  423 us

profile of v1, /device:TPU:46, one launch (start us, length us, event | category | flops | bytes accessed | tf_op | source)
XLA Modules:
  0.0 427.6 jit_solution(14014517072862085889)
XLA Ops:
  0.0 0.8 reshape.80
  0.8 0.7 fusion
  1.5 0.1 broadcast_select_fusion.refs_1_
  1.7 0.0 copy-start
  1.7 2.2 copy-done
  3.9 423.1 %shard_map.37 = f32[32,128]{1,0:T(8,128)S(1)} custom-call(bf16[4096,512]{1,0:T(8,128)(2,1)S(1)} %copy-done, s32[64,1,128]{2,1,0:T(1,128)S(1)} %broadcast_select_fusion.refs_1_), custom_call_target="tpu_custom_call" | custom-call | flops 17179869184 | bytes 8388608 | tf_op jit(solution)/shard_map/pallas_call | solution.py:230
  427.0 0.6 copy.5
  (1 shorter events, 0.0 us)
Async XLA Ops:
  1.7 2.2 copy-start

commit v2 on v1

v2 whole, which is shorter than its diff:
```python
import math

import jax
import jax.numpy as jnp
from jax import lax
from jax.experimental import pallas as pl
from jax.experimental.pallas import tpu as pltpu
from jax.sharding import PartitionSpec as P

NEAR = 4
GROUP = 4
OWNER = "owner"


def exchange_kernel(
    owners, lengths, emb_hbm, cluster_ref, out_ref,
    emb_v, land, units, lab_out, lab_land, labrow, labcol, rowacc, colbest, res_out, res_land,
    load_sem, self_sem, send_sem, recv_sem, lab_send, lab_recv, res_send, res_recv, round_sem,
):
    chips = owners // 2
    far = chips // 2
    cap = land.shape[1]
    width = land.shape[2]
    tile = 4 * cap
    half_tile = 2 * cap
    span = GROUP * tile
    last = far - 1
    me = lax.axis_index(OWNER)
    core = lax.rem(me, 2)
    chip = me // 2
    partner = chip * 2 + 1 - core
    opposite = lax.rem(chip + far, chips)

    def distance(t):
        if isinstance(t, int):
            return t + 2 if t < NEAR - 1 else 1 if t == last else far - 1 - (t - NEAR)
        raise TypeError

    def on_right(k):
        return lax.rem(chip + k, chips)

    def on_left(k):
        return lax.rem(chip + chips - k, chips)

    load = pltpu.make_async_copy(emb_hbm, emb_v, load_sem)
    load.start()

    barrier = pltpu.get_barrier_semaphore()

    def greet(k, _):
        for c in range(2):
            pl.semaphore_signal(barrier, inc=1, device_id={OWNER: on_right(k) * 2 + c})
            pl.semaphore_signal(barrier, inc=1, device_id={OWNER: on_left(k) * 2 + c})
        return 0

    pl.semaphore_signal(barrier, inc=1, device_id={OWNER: partner})
    lax.fori_loop(1, NEAR + 1, greet, 0)

    lane = lax.broadcasted_iota(jnp.int32, (1, half_tile), 1)
    slot_of = jnp.where(lane < cap, lane, lane - cap)
    for m in range(chips):
        limit = jnp.where(lane < cap, lengths[0, 2 * m], lengths[0, 2 * m + 1])
        lab_out[m] = jnp.where(slot_of < limit, cluster_ref[m:m + 1, :], -1)
    labcol[...] = jnp.full_like(labcol, -2)
    rowacc[...] = jnp.full_like(rowacc, -1.0)

    load.wait()
    pl.semaphore_wait(barrier, 4 * NEAR + 1)

    def block_copy(dest, slot, land_slot):
        return pltpu.make_async_remote_copy(
            src_ref=emb_v.at[pl.ds(pl.multiple_of(dest * cap, cap), cap)],
            dst_ref=land.at[land_slot],
            send_sem=send_sem.at[slot],
            recv_sem=recv_sem.at[land_slot],
            device_id={OWNER: dest},
        )

    def label_copy(dest, slot, land_slot):
        return pltpu.make_async_remote_copy(
            src_ref=lab_out.at[dest // 2],
            dst_ref=lab_land.at[land_slot],
            send_sem=lab_send.at[slot],
            recv_sem=lab_recv.at[land_slot],
            device_id={OWNER: dest},
        )

    def start(dest, slot, land_slot):
        label_copy(dest, slot, land_slot).start()
        block_copy(dest, slot, land_slot).start()

    def send_tile(t, k):
        for c in range(2):
            start(on_right(k) * 2 + c, t * 4 + c, t * 4 + core)
            start(on_left(k) * 2 + c, t * 4 + 2 + c, t * 4 + 2 + core)

    own = NEAR - 1
    keep = pltpu.make_async_copy(
        emb_v.at[pl.ds(pl.multiple_of(me * cap, cap), cap)], land.at[4 * own + core], self_sem.at[0])
    keep_lab = pltpu.make_async_copy(lab_out.at[chip], lab_land.at[4 * own + core], self_sem.at[1])
    keep.start()
    keep_lab.start()
    start(partner, 4 * own, 4 * own + core)
    for t in range(NEAR - 1):
        send_tile(t, distance(t))

    for r in range(far // NEAR - 1):
        pl.semaphore_signal(round_sem.at[r, 0], inc=1, device_id={OWNER: on_right(NEAR) * 2 + core})
        pl.semaphore_signal(round_sem.at[r, 1], inc=1, device_id={OWNER: on_left(NEAR) * 2 + core})
        for i in range(2):
            pl.semaphore_wait(round_sem.at[r, i], 1)

    for c in range(2):
        start(opposite * 2 + c, 4 * own + 2 + c, 4 * own + 2 + core)

    def issue(t, _):
        send_tile(t, far - 1 - (t - NEAR))
        return 0

    lax.fori_loop(NEAR, last, issue, 0)
    send_tile(last, 1)

    def take_labels(t):
        for h in range(2):
            low, high = lab_land[4 * t + 2 * h], lab_land[4 * t + 2 * h + 1]
            low = jnp.where(core == 0, low, pltpu.roll(low, cap, 1))
            high = jnp.where(core == 0, pltpu.roll(high, cap, 1), high)
            row = jnp.where(lane < cap, low, high)
            labrow[2 * t + h] = row
            column = jnp.transpose(jnp.broadcast_to(row, (half_tile, half_tile)))
            labcol[pl.ds(pl.multiple_of(t * tile + h * half_tile, half_tile), half_tile), :] = jnp.where(
                column < 0, -2, column)

    def take_rows(t):
        values = land[pl.ds(4 * t, 4)].reshape(tile, width).astype(jnp.float32)
        factor = lax.rsqrt(jnp.mean(values * values, axis=-1, keepdims=True) + 1e-06) / math.sqrt(width)
        units[pl.ds(pl.multiple_of(t * tile, tile), tile), :] = (values * factor).astype(jnp.bfloat16)

    def group(t, g, running, diagonal):
        rows = pl.ds(pl.multiple_of(g * span, span), span)
        old = units[rows, :]
        fresh = units[pl.ds(pl.multiple_of(t * tile, tile), tile), :]
        sim = lax.dot_general(
            old, fresh, (((1,), (1,)), ((), ())), preferred_element_type=jnp.float32)
        col = labcol[rows, :]
        acc = rowacc[rows, :]
        out = []
        for h in range(2):
            part = sim[:, h * half_tile:(h + 1) * half_tile]
            same = col == labrow[2 * t + h]
            if diagonal:
                i = g * span + lax.broadcasted_iota(jnp.int32, part.shape, 0)
                j = t * tile + h * half_tile + lax.broadcasted_iota(jnp.int32, part.shape, 1)
                same = same & (i != j)
            part = jnp.where(same, part, -1.0)
            acc = jnp.maximum(acc, part)
            out.append(jnp.maximum(running[h], jnp.max(part, axis=0, keepdims=True)))
        return acc, tuple(out)

    def keep_group(t, g, running, diagonal):
        acc, running = group(t, g, running, diagonal)
        rowacc[pl.ds(pl.multiple_of(g * span, span), span), :] = acc
        return running

    floor = (jnp.full((1, half_tile), -1.0, jnp.float32),) * 2

    def labels_in(slot):
        label_copy(me, slot, slot).wait_recv()

    def rows_in(slot):
        block_copy(me, slot, slot).wait_recv()

    def take_tile(t, others):
        for s in others:
            labels_in(4 * t + s)
        take_labels(t)
        for s in others:
            rows_in(4 * t + s)
        take_rows(t)

    def whole_tile(t, others=(0, 1, 2, 3)):
        take_tile(t, others)
        running = lax.fori_loop(0, t // GROUP, lambda g, r: keep_group(t, g, r, False), floor)
        running = keep_group(t, t // GROUP, running, True)
        for h in range(2):
            colbest[2 * t + h] = running[h]

    def result_copy(row, dest, slot):
        return pltpu.make_async_remote_copy(
            src_ref=res_out.at[row],
            dst_ref=res_land.at[me],
            send_sem=res_send.at[slot],
            recv_sem=res_recv.at[me],
            device_id={OWNER: dest},
        )

    def give(t, k):
        for c in range(2):
            result_copy(2 * t, on_left(k) * 2 + c, t * 4 + c).start()
            result_copy(2 * t + 1, on_right(k) * 2 + c, t * 4 + 2 + c).start()

    def step(t, _):
        whole_tile(t)
        return 0

    lax.fori_loop(0, own, step, 0)
    keep.wait()
    keep_lab.wait()
    whole_tile(own, (1 - core, 2, 3))
    lax.fori_loop(NEAR, last, step, 0)

    take_tile(last, (0, 1, 2, 3))
    square = (half_tile, half_tile)
    on_diagonal = lax.broadcasted_iota(jnp.int32, square, 0) == lax.broadcasted_iota(jnp.int32, square, 1)
    running = floor
    for g in range(far // GROUP):
        acc, running = group(last, g, running, g == last // GROUP)
        for n in range(2 * GROUP):
            i = 2 * GROUP * g + n
            best = jnp.max(acc[n * half_tile:(n + 1) * half_tile, :], axis=1, keepdims=True)
            row = jnp.max(jnp.where(on_diagonal, best, -1.0), axis=0, keepdims=True)
            old = running[n % 2] if i // 2 == last else colbest[i]
            res_out[i] = jnp.maximum(old, row)
        if g == own // GROUP:
            for c in range(2):
                result_copy(2 * own + 1, opposite * 2 + c, 4 * own + 2 + c).start()
            result_copy(2 * own, partner, 4 * own).start()
            res_land[me] = res_out[2 * own]
        for t in range(GROUP * g, GROUP * (g + 1)):
            if t != own:
                give(t, distance(t))

    def back(i, _):
        s = lax.rem(me + i, owners)
        pltpu.make_async_remote_copy(
            src_ref=res_out.at[0], dst_ref=res_land.at[s], send_sem=res_send.at[0],
            recv_sem=res_recv.at[s], device_id={OWNER: s},
        ).wait_recv()
        return 0

    lax.fori_loop(1, owners, back, 0)

    for k in range(chips):
        low, high = res_land[2 * k], res_land[2 * k + 1]
        low = jnp.where(core == 0, low, pltpu.roll(low, cap, 1))
        high = jnp.where(core == 0, pltpu.roll(high, cap, 1), high)
        out_ref[k:k + 1, :] = jnp.where(lane < cap, low, high)

    def sent(slot, _):
        block_copy(me, slot, slot).wait_send()
        label_copy(me, slot, slot).wait_send()
        result_copy(0, me, slot).wait_send()
        return 0

    lax.fori_loop(0, 4 * own + 1, sent, 0)
    lax.fori_loop(4 * own + 2, owners, sent, 0)


def on_device(embeddings, cluster, lengths):
    owners = lax.axis_size(OWNER)
    rows_here, width = embeddings.shape
    cap = rows_here // owners
    chips = owners // 2
    dma = pltpu.SemaphoreType.DMA
    out = pl.pallas_call(
        lambda *refs: exchange_kernel(owners, *refs),
        out_shape=jax.ShapeDtypeStruct((chips, 2 * cap), jnp.float32),
        in_specs=[
            pl.BlockSpec(memory_space=pltpu.SMEM),
            pl.BlockSpec(memory_space=pltpu.HBM),
            pl.BlockSpec(memory_space=pltpu.VMEM),
        ],
        out_specs=pl.BlockSpec(memory_space=pltpu.VMEM),
        scratch_shapes=[
            pltpu.VMEM((rows_here, width), jnp.bfloat16),
            pltpu.VMEM((owners, cap, width), jnp.bfloat16),
            pltpu.VMEM((rows_here, width), jnp.bfloat16),
            pltpu.VMEM((chips, 1, 2 * cap), jnp.int32),
            pltpu.VMEM((owners, 1, 2 * cap), jnp.int32),
            pltpu.VMEM((chips, 1, 2 * cap), jnp.int32),
            pltpu.VMEM((rows_here, 2 * cap), jnp.int32),
            pltpu.VMEM((rows_here, 2 * cap), jnp.float32),
            pltpu.VMEM((chips, 1, 2 * cap), jnp.float32),
            pltpu.VMEM((chips, 1, 2 * cap), jnp.float32),
            pltpu.VMEM((owners, 1, 2 * cap), jnp.float32),
            dma, dma((2,)),
            dma((owners,)), dma((owners,)), dma((owners,)), dma((owners,)), dma((owners,)), dma((owners,)),
            pltpu.SemaphoreType.REGULAR((chips // 2 // NEAR, 2)),
        ],
        compiler_params=pltpu.CompilerParams(
            collective_id=0, has_side_effects=True),
        cost_estimate=pl.CostEstimate(
            flops=2 * rows_here * rows_here * width, bytes_accessed=4 * rows_here * width, transcendentals=0),
    )(lengths, embeddings, cluster.reshape(chips, 2 * cap))
    return out.reshape(rows_here)


def solution(mesh):
    return jax.shard_map(
        on_device,
        mesh=mesh,
        in_specs=(P(("parts", OWNER), None), P(("parts", OWNER)), P(("parts", OWNER), None)),
        out_specs=P(("parts", OWNER)),
        check_vma=False,
    )
```

time: 429 us -> 421 us (0.981)
  no operation moved by 1% of the time
where the time goes in v2:
time: 421 us
  Pallas kernels  420 us (100%)
    pallas_call x1, Pallas kernels, on_device(): pl.pallas_call(lambda *refs: exchange_kernel(owners, *refs), out_shape=ja...  420 us

profile of v2, /device:TPU:46, one launch (start us, length us, event | category | flops | bytes accessed | tf_op | source)
XLA Modules:
  0.0 420.9 jit_solution(5784025296662549357)
XLA Ops:
  0.0 419.5 %shard_map.37 = f32[32,128]{1,0:T(8,128)} custom-call(s32[1,64]{1,0:T(1,128)} %refs_0_.1, bf16[4096,512]{1,0:T(8,128)(2,1)} %refs_1_.1, s32[32,128]{1,0:T(8,128)} %bitcast.3), custom_call_target="tpu_custom_call" | custom-call | flops 17179869184 | bytes 8388608 | tf_op jit(solution)/shard_map/pallas_call | solution.py:265
  419.5 1.3 copy.5

commit v3 on v2

--- a/solution.py
+++ b/solution.py
@@ -32,9 +32,7 @@
     opposite = lax.rem(chip + far, chips)
 
     def distance(t):
-        if isinstance(t, int):
-            return t + 2 if t < NEAR - 1 else 1 if t == last else far - 1 - (t - NEAR)
-        raise TypeError
+        return t + 1 if t < NEAR else far - (t - NEAR)
 
     def on_right(k):
         return lax.rem(chip + k, chips)
@@ -47,25 +45,28 @@
 
     barrier = pltpu.get_barrier_semaphore()
 
-    def greet(k, _):
-        for c in range(2):
-            pl.semaphore_signal(barrier, inc=1, device_id={OWNER: on_right(k) * 2 + c})
-            pl.semaphore_signal(barrier, inc=1, device_id={OWNER: on_left(k) * 2 + c})
-        return 0
-
-    pl.semaphore_signal(barrier, inc=1, device_id={OWNER: partner})
-    lax.fori_loop(1, NEAR + 1, greet, 0)
+    neighbours = (on_right(1) * 2 + core, on_left(1) * 2 + core, partner)
+    for neighbour in neighbours:
+        pl.semaphore_signal(barrier, inc=1, device_id={OWNER: neighbour})
+
+    def hear(r):
+        for i, neighbour in enumerate(neighbours):
+            pl.semaphore_signal(round_sem.at[r, i], inc=1, device_id={OWNER: neighbour})
+        for i in range(3):
+            pl.semaphore_wait(round_sem.at[r, i], 1)
 
     lane = lax.broadcasted_iota(jnp.int32, (1, half_tile), 1)
     slot_of = jnp.where(lane < cap, lane, lane - cap)
     for m in range(chips):
         limit = jnp.where(lane < cap, lengths[0, 2 * m], lengths[0, 2 * m + 1])
-        lab_out[m] = jnp.where(slot_of < limit, cluster_ref[m:m + 1, :], -1)
+        row = jnp.where(slot_of < limit, cluster_ref[m:m + 1, :], -1)
+        lab_out[2 * m] = row[:, :cap]
+        lab_out[2 * m + 1] = row[:, cap:]
     labcol[...] = jnp.full_like(labcol, -2)
     rowacc[...] = jnp.full_like(rowacc, -1.0)
 
     load.wait()
-    pl.semaphore_wait(barrier, 4 * NEAR + 1)
+    pl.semaphore_wait(barrier, 3)
 
     def block_copy(dest, slot, land_slot):
         return pltpu.make_async_remote_copy(
@@ -78,7 +79,7 @@
 
     def label_copy(dest, slot, land_slot):
         return pltpu.make_async_remote_copy(
-            src_ref=lab_out.at[dest // 2],
+            src_ref=lab_out.at[dest],
             dst_ref=lab_land.at[land_slot],
             send_sem=lab_send.at[slot],
             recv_sem=lab_recv.at[land_slot],
@@ -94,38 +95,31 @@
             start(on_right(k) * 2 + c, t * 4 + c, t * 4 + core)
             start(on_left(k) * 2 + c, t * 4 + 2 + c, t * 4 + 2 + core)
 
-    own = NEAR - 1
+    own = NEAR
     keep = pltpu.make_async_copy(
         emb_v.at[pl.ds(pl.multiple_of(me * cap, cap), cap)], land.at[4 * own + core], self_sem.at[0])
-    keep_lab = pltpu.make_async_copy(lab_out.at[chip], lab_land.at[4 * own + core], self_sem.at[1])
+    keep_lab = pltpu.make_async_copy(lab_out.at[me], lab_land.at[4 * own + core], self_sem.at[1])
     keep.start()
     keep_lab.start()
     start(partner, 4 * own, 4 * own + core)
-    for t in range(NEAR - 1):
+    for t in range(NEAR):
+        hear(t)
         send_tile(t, distance(t))
-
-    for r in range(far // NEAR - 1):
-        pl.semaphore_signal(round_sem.at[r, 0], inc=1, device_id={OWNER: on_right(NEAR) * 2 + core})
-        pl.semaphore_signal(round_sem.at[r, 1], inc=1, device_id={OWNER: on_left(NEAR) * 2 + core})
-        for i in range(2):
-            pl.semaphore_wait(round_sem.at[r, i], 1)
+    for r in range(NEAR, far):
+        hear(r)
 
     for c in range(2):
         start(opposite * 2 + c, 4 * own + 2 + c, 4 * own + 2 + core)
 
     def issue(t, _):
-        send_tile(t, far - 1 - (t - NEAR))
+        send_tile(t, far - (t - NEAR))
         return 0
 
-    lax.fori_loop(NEAR, last, issue, 0)
-    send_tile(last, 1)
+    lax.fori_loop(NEAR + 1, far, issue, 0)
 
     def take_labels(t):
         for h in range(2):
-            low, high = lab_land[4 * t + 2 * h], lab_land[4 * t + 2 * h + 1]
-            low = jnp.where(core == 0, low, pltpu.roll(low, cap, 1))
-            high = jnp.where(core == 0, pltpu.roll(high, cap, 1), high)
-            row = jnp.where(lane < cap, low, high)
+            row = jnp.concatenate([lab_land[4 * t + 2 * h], lab_land[4 * t + 2 * h + 1]], axis=1)
             labrow[2 * t + h] = row
             column = jnp.transpose(jnp.broadcast_to(row, (half_tile, half_tile)))
             labcol[pl.ds(pl.multiple_of(t * tile + h * half_tile, half_tile), half_tile), :] = jnp.where(
@@ -207,28 +201,35 @@
     keep.wait()
     keep_lab.wait()
     whole_tile(own, (1 - core, 2, 3))
-    lax.fori_loop(NEAR, last, step, 0)
+    lax.fori_loop(own + 1, last, step, 0)
 
     take_tile(last, (0, 1, 2, 3))
     square = (half_tile, half_tile)
     on_diagonal = lax.broadcasted_iota(jnp.int32, square, 0) == lax.broadcasted_iota(jnp.int32, square, 1)
     running = floor
-    for g in range(far // GROUP):
+    groups = far // GROUP
+    for n in range(groups):
+        g = (own // GROUP + n) % groups
         acc, running = group(last, g, running, g == last // GROUP)
-        for n in range(2 * GROUP):
-            i = 2 * GROUP * g + n
-            best = jnp.max(acc[n * half_tile:(n + 1) * half_tile, :], axis=1, keepdims=True)
+        for m in range(2 * GROUP):
+            i = 2 * GROUP * g + m
+            best = jnp.max(acc[m * half_tile:(m + 1) * half_tile, :], axis=1, keepdims=True)
             row = jnp.max(jnp.where(on_diagonal, best, -1.0), axis=0, keepdims=True)
-            old = running[n % 2] if i // 2 == last else colbest[i]
-            res_out[i] = jnp.maximum(old, row)
+            if i // 2 == last:
+                colbest[i] = row
+            else:
+                res_out[i] = jnp.maximum(colbest[i], row)
         if g == own // GROUP:
             for c in range(2):
                 result_copy(2 * own + 1, opposite * 2 + c, 4 * own + 2 + c).start()
             result_copy(2 * own, partner, 4 * own).start()
             res_land[me] = res_out[2 * own]
         for t in range(GROUP * g, GROUP * (g + 1)):
-            if t != own:
+            if t not in (own, last):
                 give(t, distance(t))
+    for h in range(2):
+        res_out[2 * last + h] = jnp.maximum(colbest[2 * last + h], running[h])
+    give(last, distance(last))
 
     def back(i, _):
         s = lax.rem(me + i, owners)
@@ -275,8 +276,8 @@
             pltpu.VMEM((rows_here, width), jnp.bfloat16),
             pltpu.VMEM((owners, cap, width), jnp.bfloat16),
             pltpu.VMEM((rows_here, width), jnp.bfloat16),
-            pltpu.VMEM((chips, 1, 2 * cap), jnp.int32),
-            pltpu.VMEM((owners, 1, 2 * cap), jnp.int32),
+            pltpu.VMEM((owners, 1, cap), jnp.int32),
+            pltpu.VMEM((owners, 1, cap), jnp.int32),
             pltpu.VMEM((chips, 1, 2 * cap), jnp.int32),
             pltpu.VMEM((rows_here, 2 * cap), jnp.int32),
             pltpu.VMEM((rows_here, 2 * cap), jnp.float32),
@@ -285,7 +286,7 @@
             pltpu.VMEM((owners, 1, 2 * cap), jnp.float32),
             dma, dma((2,)),
             dma((owners,)), dma((owners,)), dma((owners,)), dma((owners,)), dma((owners,)), dma((owners,)),
-            pltpu.SemaphoreType.REGULAR((chips // 2 // NEAR, 2)),
+            pltpu.SemaphoreType.REGULAR((chips // 2, 3)),
         ],
         compiler_params=pltpu.CompilerParams(
             collective_id=0, has_side_effects=True),

time: 421 us -> 411 us (0.976)
  Pallas kernels: 420 us -> 409 us
    pallas_call x1, Pallas kernels: 420 us -> 409 us  [on_device(): pl.pallas_call(lambda *refs: exchange_kernel(owners, *refs), out_shape=ja...]
where the time goes in v3:
time: 411 us; the launch traced here: 410 us
  Pallas kernels  409 us (100%)
    pallas_call x1, Pallas kernels, on_device(): pl.pallas_call(lambda *refs: exchange_kernel(owners, *refs), out_shape=ja...  409 us

profile of v3, /device:TPU:46, one launch (start us, length us, event | category | flops | bytes accessed | tf_op | source)
XLA Modules:
  0.0 410.1 jit_solution(12573457990015389685)
XLA Ops:
  0.0 408.7 %shard_map.37 = f32[32,128]{1,0:T(8,128)} custom-call(s32[1,64]{1,0:T(1,128)} %refs_0_.1, bf16[4096,512]{1,0:T(8,128)(2,1)} %refs_1_.1, s32[32,128]{1,0:T(8,128)} %bitcast.3), custom_call_target="tpu_custom_call" | custom-call | flops 17179869184 | bytes 8388608 | tf_op jit(solution)/shard_map/pallas_call | solution.py:266
  408.7 1.3 copy.5

commit v4 on v3

--- a/solution.py
+++ b/solution.py
@@ -45,14 +45,15 @@
 
     barrier = pltpu.get_barrier_semaphore()
 
-    neighbours = (on_right(1) * 2 + core, on_left(1) * 2 + core, partner)
-    for neighbour in neighbours:
-        pl.semaphore_signal(barrier, inc=1, device_id={OWNER: neighbour})
+    for neighbour in (on_right(1), on_left(1)):
+        for c in range(2):
+            pl.semaphore_signal(barrier, inc=1, device_id={OWNER: neighbour * 2 + c})
+    pl.semaphore_signal(barrier, inc=1, device_id={OWNER: partner})
 
     def hear(r):
-        for i, neighbour in enumerate(neighbours):
-            pl.semaphore_signal(round_sem.at[r, i], inc=1, device_id={OWNER: neighbour})
-        for i in range(3):
+        for i, neighbour in enumerate((on_right(1), on_left(1))):
+            pl.semaphore_signal(round_sem.at[r, i], inc=1, device_id={OWNER: neighbour * 2 + core})
+        for i in range(2):
             pl.semaphore_wait(round_sem.at[r, i], 1)
 
     lane = lax.broadcasted_iota(jnp.int32, (1, half_tile), 1)
@@ -66,7 +67,7 @@
     rowacc[...] = jnp.full_like(rowacc, -1.0)
 
     load.wait()
-    pl.semaphore_wait(barrier, 3)
+    pl.semaphore_wait(barrier, 5)
 
     def block_copy(dest, slot, land_slot):
         return pltpu.make_async_remote_copy(
@@ -103,9 +104,10 @@
     keep_lab.start()
     start(partner, 4 * own, 4 * own + core)
     for t in range(NEAR):
-        hear(t)
+        if t > 0:
+            hear(t - 1)
         send_tile(t, distance(t))
-    for r in range(NEAR, far):
+    for r in range(NEAR - 1, far - 1):
         hear(r)
 
     for c in range(2):
@@ -202,6 +204,14 @@
     keep_lab.wait()
     whole_tile(own, (1 - core, 2, 3))
     lax.fori_loop(own + 1, last, step, 0)
+
+    def left(slot, _):
+        block_copy(me, slot, slot).wait_send()
+        label_copy(me, slot, slot).wait_send()
+        return 0
+
+    lax.fori_loop(0, 4 * own + 1, left, 0)
+    lax.fori_loop(4 * own + 2, 4 * last, left, 0)
 
     take_tile(last, (0, 1, 2, 3))
     square = (half_tile, half_tile)
@@ -231,6 +241,14 @@
         res_out[2 * last + h] = jnp.maximum(colbest[2 * last + h], running[h])
     give(last, distance(last))
 
+    def answered(slot, _):
+        result_copy(0, me, slot).wait_send()
+        return 0
+
+    lax.fori_loop(4 * last, owners, left, 0)
+    lax.fori_loop(0, 4 * own + 1, answered, 0)
+    lax.fori_loop(4 * own + 2, owners, answered, 0)
+
     def back(i, _):
         s = lax.rem(me + i, owners)
         pltpu.make_async_remote_copy(
@@ -246,15 +264,6 @@
         low = jnp.where(core == 0, low, pltpu.roll(low, cap, 1))
         high = jnp.where(core == 0, pltpu.roll(high, cap, 1), high)
         out_ref[k:k + 1, :] = jnp.where(lane < cap, low, high)
-
-    def sent(slot, _):
-        block_copy(me, slot, slot).wait_send()
-        label_copy(me, slot, slot).wait_send()
-        result_copy(0, me, slot).wait_send()
-        return 0
-
-    lax.fori_loop(0, 4 * own + 1, sent, 0)
-    lax.fori_loop(4 * own + 2, owners, sent, 0)
 
 
 def on_device(embeddings, cluster, lengths):
@@ -286,7 +295,7 @@
             pltpu.VMEM((owners, 1, 2 * cap), jnp.float32),
             dma, dma((2,)),
             dma((owners,)), dma((owners,)), dma((owners,)), dma((owners,)), dma((owners,)), dma((owners,)),
-            pltpu.SemaphoreType.REGULAR((chips // 2, 3)),
+            pltpu.SemaphoreType.REGULAR((chips // 2 - 1, 2)),
         ],
         compiler_params=pltpu.CompilerParams(
             collective_id=0, has_side_effects=True),

time: 411 us -> 409 us (level)
  no operation moved by 1% of the time
where the time goes in v4:
time: 409 us; the launch traced here: 408 us
  Pallas kernels  407 us (100%)
    pallas_call x1, Pallas kernels, on_device(): pl.pallas_call(lambda *refs: exchange_kernel(owners, *refs), out_shape=ja...  407 us

profile of v4, /device:TPU:46, one launch (start us, length us, event | category | flops | bytes accessed | tf_op | source)
XLA Modules:
  0.0 407.9 jit_solution(15149222182104384507)
XLA Ops:
  0.0 406.5 %shard_map.37 = f32[32,128]{1,0:T(8,128)} custom-call(s32[1,64]{1,0:T(1,128)} %refs_0_.1, bf16[4096,512]{1,0:T(8,128)(2,1)} %refs_1_.1, s32[32,128]{1,0:T(8,128)} %bitcast.3), custom_call_target="tpu_custom_call" | custom-call | flops 17179869184 | bytes 8388608 | tf_op jit(solution)/shard_map/pallas_call | solution.py:275
  406.5 1.3 copy.5

commit v5 on v4

--- a/solution.py
+++ b/solution.py
@@ -14,8 +14,8 @@
 
 def exchange_kernel(
     owners, lengths, emb_hbm, cluster_ref, out_ref,
-    emb_v, land, units, lab_out, lab_land, labrow, labcol, rowacc, colbest, res_out, res_land,
-    load_sem, self_sem, send_sem, recv_sem, lab_send, lab_recv, res_send, res_recv, round_sem,
+    emb_v, first_v, land, units, lab_out, lab_other, lab_both, lab_land, labcol, rowacc, colbest, res_out, res_land,
+    load_sem, self_sem, swap_sem, send_sem, recv_sem, lab_send, lab_recv, res_send, res_recv, round_sem,
 ):
     chips = owners // 2
     far = chips // 2
@@ -40,7 +40,14 @@
     def on_left(k):
         return lax.rem(chip + chips - k, chips)
 
-    load = pltpu.make_async_copy(emb_hbm, emb_v, load_sem)
+    firsts = [
+        pltpu.make_async_copy(
+            emb_hbm.at[pl.ds(pl.multiple_of(there * half_tile, half_tile), half_tile)], first_v.at[i], load_sem.at[i])
+        for i, there in enumerate((on_right(1), on_left(1)))
+    ]
+    for first in firsts:
+        first.start()
+    load = pltpu.make_async_copy(emb_hbm, emb_v, load_sem.at[2])
     load.start()
 
     barrier = pltpu.get_barrier_semaphore()
@@ -61,13 +68,12 @@
     for m in range(chips):
         limit = jnp.where(lane < cap, lengths[0, 2 * m], lengths[0, 2 * m + 1])
         row = jnp.where(slot_of < limit, cluster_ref[m:m + 1, :], -1)
-        lab_out[2 * m] = row[:, :cap]
-        lab_out[2 * m + 1] = row[:, cap:]
-    labcol[...] = jnp.full_like(labcol, -2)
-    rowacc[...] = jnp.full_like(rowacc, -1.0)
-
-    load.wait()
+        lab_out[0, m] = row[:, :cap]
+        lab_out[1, m] = row[:, cap:]
+
     pl.semaphore_wait(barrier, 5)
+    for first in firsts:
+        first.wait()
 
     def block_copy(dest, slot, land_slot):
         return pltpu.make_async_remote_copy(
@@ -78,51 +84,80 @@
             device_id={OWNER: dest},
         )
 
-    def label_copy(dest, slot, land_slot):
+    def label_copy(there, row):
         return pltpu.make_async_remote_copy(
-            src_ref=lab_out.at[dest],
-            dst_ref=lab_land.at[land_slot],
-            send_sem=lab_send.at[slot],
-            recv_sem=lab_recv.at[land_slot],
-            device_id={OWNER: dest},
+            src_ref=lab_both.at[there],
+            dst_ref=lab_land.at[row],
+            send_sem=lab_send.at[row],
+            recv_sem=lab_recv.at[row],
+            device_id={OWNER: there * 2 + core},
         )
 
-    def start(dest, slot, land_slot):
-        label_copy(dest, slot, land_slot).start()
-        block_copy(dest, slot, land_slot).start()
-
-    def send_tile(t, k):
+    def send_rows(t, k):
         for c in range(2):
-            start(on_right(k) * 2 + c, t * 4 + c, t * 4 + core)
-            start(on_left(k) * 2 + c, t * 4 + 2 + c, t * 4 + 2 + core)
+            block_copy(on_right(k) * 2 + c, t * 4 + c, t * 4 + core).start()
+            block_copy(on_left(k) * 2 + c, t * 4 + 2 + c, t * 4 + 2 + core).start()
+
+    def send_labels(t, k):
+        label_copy(on_right(k), 2 * t).start()
+        label_copy(on_left(k), 2 * t + 1).start()
 
     own = NEAR
+    for c in range(2):
+        for i, there in enumerate((on_right(1), on_left(1))):
+            pltpu.make_async_remote_copy(
+                src_ref=first_v.at[i, pl.ds(c * cap, cap)],
+                dst_ref=land.at[2 * i + core],
+                send_sem=send_sem.at[2 * i + c],
+                recv_sem=recv_sem.at[2 * i + core],
+                device_id={OWNER: there * 2 + c},
+            ).start()
+    swap = pltpu.make_async_remote_copy(
+        src_ref=lab_out.at[1 - core],
+        dst_ref=lab_other,
+        send_sem=swap_sem.at[0],
+        recv_sem=swap_sem.at[1],
+        device_id={OWNER: partner},
+    )
+    swap.start()
+    load.wait()
+    for t in range(1, NEAR):
+        hear(t - 1)
+        send_rows(t, distance(t))
     keep = pltpu.make_async_copy(
-        emb_v.at[pl.ds(pl.multiple_of(me * cap, cap), cap)], land.at[4 * own + core], self_sem.at[0])
-    keep_lab = pltpu.make_async_copy(lab_out.at[me], lab_land.at[4 * own + core], self_sem.at[1])
+        emb_v.at[pl.ds(pl.multiple_of(me * cap, cap), cap)], land.at[4 * own + core], self_sem)
     keep.start()
-    keep_lab.start()
-    start(partner, 4 * own, 4 * own + core)
-    for t in range(NEAR):
-        if t > 0:
-            hear(t - 1)
-        send_tile(t, distance(t))
+    block_copy(partner, 4 * own, 4 * own + core).start()
+
+    swap.wait()
+    for m in range(chips):
+        mine, other = lab_out[core, m], lab_other[m]
+        lab_both[m] = jnp.concatenate(
+            [jnp.where(core == 0, mine, other), jnp.where(core == 0, other, mine)], axis=1)
+    lab_land[2 * own] = lab_both[chip]
+
     for r in range(NEAR - 1, far - 1):
         hear(r)
-
+    for t in range(NEAR):
+        send_labels(t, distance(t))
+
+    label_copy(opposite, 2 * own + 1).start()
     for c in range(2):
-        start(opposite * 2 + c, 4 * own + 2 + c, 4 * own + 2 + core)
+        block_copy(opposite * 2 + c, 4 * own + 2 + c, 4 * own + 2 + core).start()
 
     def issue(t, _):
-        send_tile(t, far - (t - NEAR))
+        send_labels(t, far - (t - NEAR))
+        send_rows(t, far - (t - NEAR))
         return 0
 
     lax.fori_loop(NEAR + 1, far, issue, 0)
+
+    labcol[...] = jnp.full_like(labcol, -2)
+    rowacc[...] = jnp.full_like(rowacc, -1.0)
 
     def take_labels(t):
         for h in range(2):
-            row = jnp.concatenate([lab_land[4 * t + 2 * h], lab_land[4 * t + 2 * h + 1]], axis=1)
-            labrow[2 * t + h] = row
+            row = lab_land[2 * t + h]
             column = jnp.transpose(jnp.broadcast_to(row, (half_tile, half_tile)))
             labcol[pl.ds(pl.multiple_of(t * tile + h * half_tile, half_tile), half_tile), :] = jnp.where(
                 column < 0, -2, column)
@@ -143,7 +178,7 @@
         out = []
         for h in range(2):
             part = sim[:, h * half_tile:(h + 1) * half_tile]
-            same = col == labrow[2 * t + h]
+            same = col == lab_land[2 * t + h]
             if diagonal:
                 i = g * span + lax.broadcasted_iota(jnp.int32, part.shape, 0)
                 j = t * tile + h * half_tile + lax.broadcasted_iota(jnp.int32, part.shape, 1)
@@ -160,22 +195,22 @@
 
     floor = (jnp.full((1, half_tile), -1.0, jnp.float32),) * 2
 
-    def labels_in(slot):
-        label_copy(me, slot, slot).wait_recv()
+    def labels_in(row):
+        label_copy(chip, row).wait_recv()
 
     def rows_in(slot):
         block_copy(me, slot, slot).wait_recv()
 
-    def take_tile(t, others):
-        for s in others:
-            labels_in(4 * t + s)
+    def take_tile(t, others, halves):
+        for h in halves:
+            labels_in(2 * t + h)
         take_labels(t)
         for s in others:
             rows_in(4 * t + s)
         take_rows(t)
 
-    def whole_tile(t, others=(0, 1, 2, 3)):
-        take_tile(t, others)
+    def whole_tile(t, others=(0, 1, 2, 3), halves=(0, 1)):
+        take_tile(t, others, halves)
         running = lax.fori_loop(0, t // GROUP, lambda g, r: keep_group(t, g, r, False), floor)
         running = keep_group(t, t // GROUP, running, True)
         for h in range(2):
@@ -201,19 +236,24 @@
 
     lax.fori_loop(0, own, step, 0)
     keep.wait()
-    keep_lab.wait()
-    whole_tile(own, (1 - core, 2, 3))
+    whole_tile(own, (1 - core, 2, 3), (1,))
     lax.fori_loop(own + 1, last, step, 0)
 
     def left(slot, _):
         block_copy(me, slot, slot).wait_send()
-        label_copy(me, slot, slot).wait_send()
-        return 0
+        return 0
+
+    def told(row, _):
+        label_copy(chip, row).wait_send()
+        return 0
+
+    lax.fori_loop(0, 2 * own, told, 0)
+    lax.fori_loop(2 * own + 1, chips, told, 0)
 
     lax.fori_loop(0, 4 * own + 1, left, 0)
     lax.fori_loop(4 * own + 2, 4 * last, left, 0)
 
-    take_tile(last, (0, 1, 2, 3))
+    take_tile(last, (0, 1, 2, 3), (0, 1))
     square = (half_tile, half_tile)
     on_diagonal = lax.broadcasted_iota(jnp.int32, square, 0) == lax.broadcasted_iota(jnp.int32, square, 1)
     running = floor
@@ -283,18 +323,20 @@
         out_specs=pl.BlockSpec(memory_space=pltpu.VMEM),
         scratch_shapes=[
             pltpu.VMEM((rows_here, width), jnp.bfloat16),
+            pltpu.VMEM((2, 2 * cap, width), jnp.bfloat16),
             pltpu.VMEM((owners, cap, width), jnp.bfloat16),
             pltpu.VMEM((rows_here, width), jnp.bfloat16),
-            pltpu.VMEM((owners, 1, cap), jnp.int32),
-            pltpu.VMEM((owners, 1, cap), jnp.int32),
+            pltpu.VMEM((2, chips, 1, cap), jnp.int32),
+            pltpu.VMEM((chips, 1, cap), jnp.int32),
+            pltpu.VMEM((chips, 1, 2 * cap), jnp.int32),
             pltpu.VMEM((chips, 1, 2 * cap), jnp.int32),
             pltpu.VMEM((rows_here, 2 * cap), jnp.int32),
             pltpu.VMEM((rows_here, 2 * cap), jnp.float32),
             pltpu.VMEM((chips, 1, 2 * cap), jnp.float32),
             pltpu.VMEM((chips, 1, 2 * cap), jnp.float32),
             pltpu.VMEM((owners, 1, 2 * cap), jnp.float32),
-            dma, dma((2,)),
-            dma((owners,)), dma((owners,)), dma((owners,)), dma((owners,)), dma((owners,)), dma((owners,)),
+            dma((3,)), dma, dma((2,)),
+            dma((owners,)), dma((owners,)), dma((chips,)), dma((chips,)), dma((owners,)), dma((owners,)),
             pltpu.SemaphoreType.REGULAR((chips // 2 - 1, 2)),
         ],
         compiler_params=pltpu.CompilerParams(

time: 409 us -> 407 us (level)
  no operation moved by 1% of the time
where the time goes in v5:
time: 407 us; the launch traced here: 406 us
  Pallas kernels  404 us (99%)
    pallas_call x1, Pallas kernels, on_device(): pl.pallas_call(lambda *refs: exchange_kernel(owners, *refs), out_shape=ja...  404 us

profile of v5, /device:TPU:46, one launch (start us, length us, event | category | flops | bytes accessed | tf_op | source)
XLA Modules:
  0.0 405.6 jit_solution(1266285673221019758)
XLA Ops:
  0.0 404.3 %shard_map.37 = f32[32,128]{1,0:T(8,128)} custom-call(s32[1,64]{1,0:T(1,128)} %refs_0_.1, bf16[4096,512]{1,0:T(8,128)(2,1)} %refs_1_.1, s32[32,128]{1,0:T(8,128)} %bitcast.3), custom_call_target="tpu_custom_call" | custom-call | flops 17179869184 | bytes 8388608 | tf_op jit(solution)/shard_map/pallas_call | solution.py:315
  404.3 1.3 copy.5

commit v6 on v5

--- a/solution.py
+++ b/solution.py
@@ -7,7 +7,7 @@
 from jax.experimental.pallas import tpu as pltpu
 from jax.sharding import PartitionSpec as P
 
-NEAR = 4
+NEAR = 3
 GROUP = 4
 OWNER = "owner"
 
@@ -32,7 +32,7 @@
     opposite = lax.rem(chip + far, chips)
 
     def distance(t):
-        return t + 1 if t < NEAR else far - (t - NEAR)
+        return 1 if t == 0 else 2 if t == last else t + 2 if t < NEAR else far - (t - NEAR)
 
     def on_right(k):
         return lax.rem(chip + k, chips)
@@ -121,8 +121,11 @@
     )
     swap.start()
     load.wait()
+    heard = 0
     for t in range(1, NEAR):
-        hear(t - 1)
+        for r in range(heard, distance(t) - 1):
+            hear(r)
+        heard = distance(t) - 1
         send_rows(t, distance(t))
     keep = pltpu.make_async_copy(
         emb_v.at[pl.ds(pl.multiple_of(me * cap, cap), cap)], land.at[4 * own + core], self_sem)
@@ -136,7 +139,7 @@
             [jnp.where(core == 0, mine, other), jnp.where(core == 0, other, mine)], axis=1)
     lab_land[2 * own] = lab_both[chip]
 
-    for r in range(NEAR - 1, far - 1):
+    for r in range(heard, far - 1):
         hear(r)
     for t in range(NEAR):
         send_labels(t, distance(t))
@@ -150,7 +153,9 @@
         send_rows(t, far - (t - NEAR))
         return 0
 
-    lax.fori_loop(NEAR + 1, far, issue, 0)
+    lax.fori_loop(NEAR + 1, last, issue, 0)
+    send_labels(last, distance(last))
+    send_rows(last, distance(last))
 
     labcol[...] = jnp.full_like(labcol, -2)
     rowacc[...] = jnp.full_like(rowacc, -1.0)

time: 407 us -> 408 us (level)
  no operation moved by 1% of the time
where the time goes in v6:
time: 408 us
  Pallas kernels  406 us (100%)
    pallas_call x1, Pallas kernels, on_device(): pl.pallas_call(lambda *refs: exchange_kernel(owners, *refs), out_shape=ja...  406 us

profile of v6, /device:TPU:46, one launch (start us, length us, event | category | flops | bytes accessed | tf_op | source)
XLA Modules:
  0.0 407.7 jit_solution(10944883125137098963)
XLA Ops:
  0.0 406.3 %shard_map.37 = f32[32,128]{1,0:T(8,128)} custom-call(s32[1,64]{1,0:T(1,128)} %refs_0_.1, bf16[4096,512]{1,0:T(8,128)(2,1)} %refs_1_.1, s32[32,128]{1,0:T(8,128)} %bitcast.3), custom_call_target="tpu_custom_call" | custom-call | flops 17179869184 | bytes 8388608 | tf_op jit(solution)/shard_map/pallas_call | solution.py:320
  406.3 1.3 copy.5
